TPU v7x, 32 devices: a whole 2x2x4 slice. The times are simulated.
32 devices in a mesh: gz: 4 (over z), gx: 4 (over y, x), gy: 2 (over core).
Axes of the slice: x: 2, y: 2, z: 4, core: 2. Of those that a mesh axis runs over, the one named last changes fastest.
Arguments:
- density: float32 [128, 256, 1024], P('gz', 'gy', 'gx'), may hold values from 0 to 1
- mask: int32 [16, 32, 128], P('gz', 'gy', 'gx'), may hold values from 0 to 3
Outputs:
- filtered: float32 [128, 256, 1024], P(('gz', 'gx'), 'gy')
- projected: float32 [128, 256, 1024], P(('gz', 'gx'), 'gy')
Inputs may be any that keep to these rules, and one draw needn't show every extreme that they name: `mask`: code 0 marks a void block, 1 a solid block, 2 and 3 design blocks.
All inputs are finite; a program needn't handle non-finite values.
Results may differ from a plain program's by a relative error of at most 0.0003.
Values sent between devices are 32-bit elements; how exact they have to be, the bound alone decides.
A program may use at most 128 MiB of HBM per device.

v0:
```python
import jax
import jax.numpy as jnp
from jax import lax
from jax.sharding import PartitionSpec as P

RADIUS = 6
CELLS = 8


sharpness = 8.0
threshold = 0.5
highest = lax.Precision.HIGHEST


def with_halo(x, sides, width):
    for axis, dim in sides:
        peers, length = (lax.axis_size(axis), x.shape[dim])
        up = [(i, (i + 1) % peers) for i in range(peers - 1)]
        down = [(j, i) for i, j in up]
        last = lax.slice_in_dim(x, length - width, length, axis=dim)
        leading = lax.slice_in_dim(x, 0, width, axis=dim)
        before = lax.ppermute(last, axis, up)
        after = lax.ppermute(leading, axis, down)
        x = jnp.concatenate([before, x, after], axis=dim)
    return x


def passed_along(block, axis, distance):
    devices = range(lax.axis_size(axis))
    route = [(i - distance, i) for i in devices if i - distance in devices]
    return lax.ppermute(block, axis, route)


def band(outputs, inputs, shift):
    out_index = lax.broadcasted_iota(jnp.int32, (outputs, inputs), 0)
    in_index = lax.broadcasted_iota(jnp.int32, (outputs, inputs), 1)
    distance = jnp.abs(in_index + shift - out_index)
    return jnp.where(distance <= RADIUS, (RADIUS + 1 - distance).astype(jnp.float32), 0.0)


def along_first(extended, count):
    kernel = band(count, count + 2 * RADIUS, -RADIUS)
    flat = extended.reshape(count + 2 * RADIUS, -1)
    result = jnp.dot(kernel, flat, precision=highest, preferred_element_type=jnp.float32)
    return result.reshape((count,) + extended.shape[1:])


def filter_last(values):
    leading = values.shape[:-1]
    extent = values.shape[-1]
    blocks = extent // 128
    widths = [(0, 0)] * (values.ndim - 1) + [(RADIUS, 128 - RADIUS)]
    padded = jnp.pad(values, widths)
    lower_part = padded[..., :extent].reshape(leading + (blocks, 128))
    upper_part = padded[..., 128 : extent + 128].reshape(leading + (blocks, 128))[..., : 2 * RADIUS]
    lower_kernel = band(128, 128, -RADIUS).T
    upper_kernel = band(128, 2 * RADIUS, 128 - RADIUS).T
    result = jnp.einsum(
        "abcd,de->abce",
        lower_part,
        lower_kernel,
        precision=highest,
        preferred_element_type=jnp.float32,
    )
    result = result + jnp.einsum(
        "abcd,de->abce",
        upper_part,
        upper_kernel,
        precision=highest,
        preferred_element_type=jnp.float32,
    )
    return result.reshape(leading + (extent,))


def one_side(reach):
    return reach * (RADIUS + 1) - reach * (reach + 1) // 2


def edge_sums(start, length, length_all):
    position = start + lax.iota(jnp.int32, length)
    reach_left = jnp.minimum(position, RADIUS)
    reach_right = jnp.minimum(length_all - 1 - position, RADIUS)
    return (RADIUS + 1 + one_side(reach_left) + one_side(reach_right)).astype(jnp.float32)


def body(density, mask):
    planes, row_count, columns = density.shape
    design_code = jnp.repeat(jnp.repeat(jnp.repeat(mask, CELLS, 0), CELLS, 1), CELLS, 2)
    physical = jnp.where(design_code == 0, 0.0, jnp.where(design_code == 1, 1.0, density))
    extended = with_halo(physical, (("gz", 0),), RADIUS)
    physical = along_first(extended, planes)
    groups = lax.axis_size("gx")
    layers = planes // groups
    gathered = lax.all_gather(physical, "gx", axis=2, tiled=True)
    own_slab = lax.dynamic_slice_in_dim(gathered, lax.axis_index("gx") * layers, layers, 0)
    smoothed = filter_last(own_slab)
    row_kernel = band(row_count + 2 * RADIUS, row_count, RADIUS)
    partial_value = jnp.einsum(
        "wy,zyx->zwx", row_kernel, smoothed, precision=highest, preferred_element_type=jnp.float32
    )
    from_previous = passed_along(partial_value[:, row_count + RADIUS :], "gy", 1)
    from_next = passed_along(partial_value[:, :RADIUS], "gy", -1)
    summed = partial_value[:, RADIUS : row_count + RADIUS]
    summed = summed.at[:, :RADIUS].add(from_previous)
    summed = summed.at[:, row_count - RADIUS :].add(from_next)
    width_all = summed.shape[2]
    count_x = edge_sums(0, width_all, width_all)
    count_y = edge_sums(
        lax.axis_index("gy") * row_count, row_count, row_count * lax.axis_size("gy")
    )
    count_z = edge_sums(lax.axis_index(("gz", "gx")) * layers, layers, planes * lax.axis_size("gz"))
    counts = count_z[:, None, None] * count_y[None, :, None] * count_x[None, None, :]
    filtered = summed / counts
    top = jnp.tanh(sharpness * threshold)
    projected = (top + jnp.tanh(sharpness * (filtered - threshold))) / (
        top + jnp.tanh(sharpness * (1.0 - threshold))
    )
    return (filtered, projected)


def solution(mesh):
    placed = (P("gz", "gy", "gx"), P("gz", "gy", "gx"))
    return jax.shard_map(
        body,
        mesh=mesh,
        in_specs=placed,
        out_specs=(P(("gz", "gx"), "gy", None), P(("gz", "gx"), "gy", None)),
        check_vma=False,
    )
```

profile of v0, /device:TPU:0, one launch (start us, length us, event | category | flops | bytes accessed | tf_op | source)
XLA Modules:
  0.0 268.2 jit_solution(17952805797014648781)
XLA Ops:
  7.2 0.0 copy-start
  7.2 0.0 all-gather.2.cloned.1.call-start
  7.2 5.6 %copy.16 = f32[32,128,256]{1,2,0:T(8,128)} copy(f32[32,128,256]{2,1,0:T(8,128)} %param.6) | data formatting | bytes 8388608 | tf_op args[0]
  12.8 0.0 copy-done
  12.8 0.3 broadcast_bitcast_fusion
  13.1 0.6 copy.15
  13.8 0.3 broadcast_bitcast_fusion.1
  14.1 0.6 copy.14
  14.8 3.3 %select_select_fusion = f32[32,128,256]{1,2,0:T(8,128)S(1)} fusion(f32[32,128,256]{1,2,0:T(8,128)} %copy.16, pred[32,128,32]{1,2,0:T(8,128)(4,1)S(1)} %copy.15, pred[32,128,32]{1,2,0:T(8,128)(4,1)S(1)} %copy.14), kind=kLoop, calls=%fused_computation.14 | loop fusion | flops 2097152 | bytes 8650752 | tf_op jit(solution)/shard_map/jit(_where)/select_n | solution.py:89
  18.0 0.1 fusion.86
  18.2 1.3 collective-permute-start.1
  19.5 5.6 %collective-permute-start = (f32[6,128,256]{1,2,0:T(8,128)S(1)}, f32[6,128,256]{1,2,0:T(8,128)S(1)}, u32[]{:S(2)}, u32[]{:S(2)}) collective-permute-start(f32[6,128,256]{1,2,0:T(8,128)S(1)} %get-tuple-element.32), channel_id=1, source_target_pairs={{0,8},{8,16},{16,24},{1,9},{9,17},{17,25},{2,10},{10,18},{18,26},{... | collective-permute-start | bytes 2359304 | tf_op jit(solution)/shard_map/ppermute | solution.py:22
  25.1 15.5 %collective-permute-done.1 = f32[6,128,256]{1,2,0:T(8,128)S(1)} collective-permute-done((f32[6,128,256]{1,2,0:T(8,128)S(1)}, f32[6,128,256]{1,2,0:T(8,128)S(1)}, u32[]{:S(2)}, u32[]{:S(2)}) %collective-permute-start.1) | collective-permute-done | bytes 786464 | tf_op jit(solution)/shard_map/ppermute | solution.py:23
  40.6 1.2 collective-permute-done
  41.8 2.9 %pad_maximum_fusion = f32[44,128,256]{1,2,0:T(8,128)} fusion(f32[6,128,256]{1,2,0:T(8,128)S(1)} %collective-permute-done.1, f32[32,128,256]{1,2,0:T(8,128)S(1)} %select_select_fusion, f32[6,128,256]{1,2,0:T(8,128)S(1)} %collective-permute-done), kind=kLoop, calls=%fused_computation.3 | loop fusion | flops 2883584 | bytes 11534336 | tf_op jit(solution)/shard_map/concatenate | solution.py:24
  44.7 6.3 %copy.17 = f32[44,128,256]{2,1,0:T(8,128)} copy(f32[44,128,256]{1,2,0:T(8,128)} %pad_maximum_fusion) | data formatting | bytes 11534336 | tf_op jit(solution)/shard_map/concatenate | solution.py:24
  51.0 3.3 %slice_bitcast_fusion = f32[128,256,44]{1,0,2:T(8,128)S(1)} fusion(f32[44,128,256]{2,1,0:T(8,128)} %copy.17), kind=kLoop, calls=%fused_computation.2 | loop fusion | bytes 11534336 | tf_op jit(solution)/shard_map/dot_general | solution.py:44
  54.3 8.2 %fusion = f32[32,128,256]{2,0,1:T(8,128)} fusion(f32[128,256,44]{1,0,2:T(8,128)S(1)} %slice_bitcast_fusion, s32[44]{0:T(128)S(1)} %iota_add_fusion.3), kind=kOutput, calls=%fused_computation | convolution fusion | flops 553656576 | bytes 9961648 | tf_op jit(solution)/shard_map/dot_general | solution.py:44
  62.4 0.0 all-gather.2.cloned.1.call-update
  62.6 159.6 %all-gather.2.cloned.1.call-done = f32[32,128,1024]{2,0,1:T(8,128)} async-done(((f32[32,128,256]{2,0,1:T(8,128)}), f32[32,128,1024]{2,0,1:T(8,128)}) %all-gather.2.cloned.1.call-update) | async-done | bytes 16777232 | tf_op jit(solution)/shard_map/all_gather | solution.py:94
  222.1 2.5 constant_dynamic-slice_fusion
  224.6 2.2 fusion.2
  226.9 6.4 %fusion.4 = f32[8,128,8,128]{1,3,2,0:T(8,128)S(1)} fusion(f32[8,128,8,12]{3,0,2,1:T(8,128)S(1)} %bitcast.47, s32[12]{0:T(128)S(1)} %iota_add_fusion.1), kind=kOutput, calls=%fused_computation.8 | convolution fusion | flops 151004160 | bytes 4587568 | tf_op jit(solution)/shard_map/abcd,de->abce/dot_general | solution.py:65
  233.3 6.5 %fusion.8 = f32[8,128,8,128]{1,3,2,0:T(8,128)S(1)} fusion(f32[8,128,8,128]{1,3,2,0:T(8,128)S(1)} %fusion.4, f32[8,128,8,128]{3,0,2,1:T(8,128)S(1)} %get-tuple-element.30, s32[128]{0:T(128)S(1)} %iota_add_fusion.2), kind=kOutput, calls=%fused_computation.16 | convolution fusion | flops 1611759616 | bytes 12583424 | tf_op jit(solution)/shard_map/abcd,de->abce/dot_general | solution.py:58
  239.8 4.4 %convolution_bitcast_fusion = f32[8,140,1024]{2,1,0:T(8,128)S(1)} fusion(f32[8,128,1024]{1,2,0:T(8,128)S(1)} %bitcast.48, s32[128]{0:T(128)S(1)} %iota_add_fusion), kind=kOutput, calls=%fused_computation.15 | convolution fusion | flops 1761715200 | bytes 8782336 | tf_op jit(solution)/shard_map/wy,zyx->zwx/dot_general | solution.py:98
  244.2 0.1 fusion.85
  244.2 1.6 collective-permute-start.2
  245.8 0.1 broadcast_multiply_fusion
  245.9 2.5 slice.86
  248.5 1.3 collective-permute-start.3
  249.7 0.0 collective-permute-done.2
  249.8 1.8 scatter-add.6
  251.6 0.3 collective-permute-done.3
  251.9 1.0 slice_add_fusion
  252.9 1.7 scatter-add.9
  254.6 6.8 %add_multiply_fusion = (f32[8,128,1024]{2,1,0:T(8,128)}, f32[8,128,1024]{2,1,0:T(8,128)}) fusion(f32[8,128,1024]{2,1,0:T(8,128)} %scatter-add.9, f32[1024]{0:T(1024)S(1)} %fusion.56, f32[8,128]{1,0:T(8,128)S(1)} %broadcast_multiply_fusion), kind=kLoop, calls=%fused_computation.12 | loop fusion | flops 6291456 | bytes 12591104 | tf_op jit(solution)/shard_map/div | solution.py:115
  (11 shorter events, 0.2 us)
Async XLA Ops:
  7.2 5.6 %copy-start = (s32[4,16,32]{2,1,0:T(8,128)S(1)}, s32[4,16,32]{2,1,0:T(8,128)}, u32[]{:S(2)}) copy-start(s32[4,16,32]{2,1,0:T(8,128)} %param.7) | copy-start | bytes 24580
  7.2 215.0 %all-gather.2.cloned.1.call-start = ((), (), s32[]{:S(2)}) async-start(), calls=%async_computation | async-start | bytes 20971520 | tf_op jit(solution)/shard_map/all_gather | solution.py:94
  18.2 22.5 %collective-permute-start.1 = (f32[6,128,256]{1,2,0:T(8,128)S(1)}, f32[6,128,256]{1,2,0:T(8,128)S(1)}, u32[]{:S(2)}, u32[]{:S(2)}) collective-permute-start(f32[6,128,256]{1,2,0:T(8,128)S(1)} %get-tuple-element.33), channel_id=1, source_target_pairs={{8,0},{16,8},{24,16},{9,1},{17,9},{25,17},{10,2},{18,10},{26,18},{... | collective-permute-start | bytes 2359304 | tf_op jit(solution)/shard_map/ppermute | solution.py:23
  19.5 22.4 %collective-permute-start = (f32[6,128,256]{1,2,0:T(8,128)S(1)}, f32[6,128,256]{1,2,0:T(8,128)S(1)}, u32[]{:S(2)}, u32[]{:S(2)}) collective-permute-start(f32[6,128,256]{1,2,0:T(8,128)S(1)} %get-tuple-element.32), channel_id=1, source_target_pairs={{0,8},{8,16},{16,24},{1,9},{9,17},{17,25},{2,10},{10,18},{18,26},{... | collective-permute-start | bytes 2359304 | tf_op jit(solution)/shard_map/ppermute | solution.py:22
  244.2 5.5 %collective-permute-start.2 = (f32[8,6,1024]{2,1,0:T(8,128)S(1)}, f32[8,6,1024]{2,1,0:T(8,128)S(1)}, u32[]{:S(2)}, u32[]{:S(2)}) collective-permute-start(f32[8,6,1024]{2,1,0:T(8,128)S(1)} %get-tuple-element.29), channel_id=1, source_target_pairs={{0,1},{2,3},{4,5},{6,7},{8,9},{10,11},{12,13},{14,15},{16,17},{18,... | collective-permute-start | bytes 589832 | tf_op jit(solution)/shard_map/ppermute | solution.py:31
  248.5 3.4 %collective-permute-start.3 = (f32[8,6,1024]{2,1,0:T(8,128)S(1)}, f32[8,6,1024]{2,1,0:T(8,128)S(1)}, u32[]{:S(2)}, u32[]{:S(2)}) collective-permute-start(f32[8,6,1024]{2,1,0:T(8,128)S(1)} %get-tuple-element.28), channel_id=1, source_target_pairs={{1,0},{3,2},{5,4},{7,6},{9,8},{11,10},{13,12},{15,14},{17,16},{19,... | collective-permute-start | bytes 589832 | tf_op jit(solution)/shard_map/ppermute | solution.py:31
Sparse Core Ops, SparseCore 0:
  62.6 159.5 all-gather.1
where the time goes:
time: 269 us; the launch traced here: 268 us
  waiting for transfers between devices  177 us (66%)
  local copies, waits for them, and re-layouts  28 us (10%)
  matrix products  25.5 us (9%)
  between operations  14.2 us (5%)
  other arithmetic  14.1 us (5%)
  starting transfers between devices  9.83 us (4%)
    all_gather x1, waiting for transfers between devices, body(): gathered = lax.all_gather(physical, 'gx', axis=2, tiled=True)  160 us
    ppermute x1, waiting for transfers between devices, with_halo(): after = lax.ppermute(leading, axis, down)  15.5 us
    dot_general x1, matrix products, along_first(): jnp.dot(kernel, flat, precision=highest, preferred_element_type=jnp.float32)  8.17 us
    div x1, other arithmetic, body(): (top + jnp.tanh(sharpness * (filtered - threshold))) / (top + jnp.tanh(sh...  6.76 us
    dot_general x1, matrix products, filter_last(): jnp.einsum('abcd,de->abce', lower_part, lower_kernel, precision=highest,...  6.49 us
    dot_general x1, matrix products, filter_last(): jnp.einsum('abcd,de->abce', upper_part, upper_kernel, precision=highest,...  6.43 us
    concatenate x1, local copies, waits for them, and re-layouts, with_halo(): x = jnp.concatenate([before, x, after], axis=dim)  6.27 us
    ppermute x1, starting transfers between devices, with_halo(): before = lax.ppermute(last, axis, up)  5.63 us
  transfers between devices with their start and end apart: 5, of which 4 were waited for; matrix products, arithmetic and copies ran while one was open for 2% of the time, Pallas kernels for 0%

commit v1 on v0

v1 whole, which is shorter than its diff:
```python
import functools
import math

import jax
import jax.numpy as jnp
from jax import lax
from jax.experimental import pallas as pl
from jax.experimental.pallas import tpu as pltpu
from jax.sharding import PartitionSpec as P

RADIUS = 6
CELLS = 8
LANES = 128
SUBLANES = 8

sharpness = 8.0
threshold = 0.5
MESH = pl.DeviceIdType.MESH


def hat(rows, cols, offset):
    row = lax.broadcasted_iota(jnp.int32, (rows, cols), 0)
    col = lax.broadcasted_iota(jnp.int32, (rows, cols), 1)
    return jnp.maximum(RADIUS + 1 - jnp.abs(col + offset - row), 0).astype(jnp.float32)


def halves(values):
    high = values.astype(jnp.bfloat16)
    low = (values - high.astype(jnp.float32)).astype(jnp.bfloat16)
    return high, low


def dot(a, b):
    return jnp.dot(a, b, preferred_element_type=jnp.float32)


def kernel(
    sizes,
    density,
    mask,
    out,
    phys,
    codes,
    masks,
    zf,
    recv,
    yb,
    xs,
    stage,
    w_own,
    w_edge,
    load_sem,
    mask_sem,
    hmask_send,
    hmask_recv,
    halo_send,
    halo_recv,
    send_sem,
    recv_sem,
    y_send,
    y_recv,
    out_sem,
):
    nz, nx, ny = sizes
    planes, rows, columns = density.shape
    blocks = mask.shape[0]
    layers = planes // nx
    gz, gx, gy = lax.axis_index("gz"), lax.axis_index("gx"), lax.axis_index("gy")
    has_up, has_down = gz > 0, gz < nz - 1
    has_prev, has_next = gy > 0, gy < ny - 1

    def load(b):
        part = pl.ds(b * CELLS, CELLS)
        return pltpu.make_async_copy(
            density.at[part], phys.at[pl.ds(RADIUS + b * CELLS, CELLS)], load_sem.at[b]
        )

    mask_copy = pltpu.make_async_copy(mask, masks.at[pl.ds(1, blocks)], mask_sem)
    mask_copy.start()
    for b in range(blocks):
        load(b).start()

    barrier = pltpu.get_barrier_semaphore()

    def greet(**where):
        pl.semaphore_signal(barrier, inc=1, device_id=where, device_id_type=MESH)

    pl.when(has_up)(lambda: greet(gz=gz - 1))
    pl.when(has_down)(lambda: greet(gz=gz + 1))
    pl.when(has_prev)(lambda: greet(gy=gy - 1))
    pl.when(has_next)(lambda: greet(gy=gy + 1))
    for step in range(1, nx):
        greet(gx=lax.rem(gx + step, nx))

    w_own[...] = hat(columns, columns, 0).astype(jnp.bfloat16)
    w_edge[pl.ds(0, LANES)] = hat(LANES, columns, LANES).astype(jnp.bfloat16)
    w_edge[pl.ds(LANES, LANES)] = hat(LANES, columns, -columns).astype(jnp.bfloat16)
    count = (
        nx
        - 1
        + has_up.astype(jnp.int32)
        + has_down.astype(jnp.int32)
        + has_prev.astype(jnp.int32)
        + has_next.astype(jnp.int32)
    )
    pl.semaphore_wait(barrier, count)

    def to_next(j):
        return pltpu.make_async_remote_copy(
            src_ref=density.at[planes - 1 - j],
            dst_ref=phys.at[RADIUS - 1 - j],
            send_sem=halo_send.at[0, j],
            recv_sem=halo_recv.at[0, j],
            device_id={"gz": gz + 1},
            device_id_type=MESH,
        )

    def to_previous(j):
        return pltpu.make_async_remote_copy(
            src_ref=density.at[j],
            dst_ref=phys.at[RADIUS + planes + j],
            send_sem=halo_send.at[1, j],
            recv_sem=halo_recv.at[1, j],
            device_id={"gz": gz - 1},
            device_id_type=MESH,
        )

    def mask_next():
        return pltpu.make_async_remote_copy(
            src_ref=mask.at[blocks - 1],
            dst_ref=masks.at[0],
            send_sem=hmask_send.at[0],
            recv_sem=hmask_recv.at[0],
            device_id={"gz": gz + 1},
            device_id_type=MESH,
        )

    def mask_previous():
        return pltpu.make_async_remote_copy(
            src_ref=mask.at[0],
            dst_ref=masks.at[blocks + 1],
            send_sem=hmask_send.at[1],
            recv_sem=hmask_recv.at[1],
            device_id={"gz": gz - 1},
            device_id_type=MESH,
        )

    @pl.when(has_down)
    def _():
        mask_next().start()
        for j in range(RADIUS):
            to_next(j).start()

    @pl.when(has_up)
    def _():
        mask_previous().start()
        for j in range(RADIUS):
            to_previous(j).start()

    def spread(b):
        small = masks[b].astype(jnp.float32).astype(jnp.bfloat16)
        mrows, mcols = small.shape
        r = lax.broadcasted_iota(jnp.int32, (rows, mrows), 0) // CELLS
        m = lax.broadcasted_iota(jnp.int32, (rows, mrows), 1)
        tall = dot(jnp.where(r == m, 1.0, 0.0).astype(jnp.bfloat16), small)
        c = lax.broadcasted_iota(jnp.int32, (mcols, columns), 1) // CELLS
        n = lax.broadcasted_iota(jnp.int32, (mcols, columns), 0)
        wide = jnp.where(c == n, 1.0, 0.0).astype(jnp.bfloat16)
        codes[b] = dot(tall.astype(jnp.bfloat16), wide)

    def apply_mask(row, b):
        code = codes[b]
        phys[row] = jnp.where(code < 0.5, 0.0, jnp.where(code < 1.5, 1.0, phys[row]))

    mask_copy.wait()
    for b in range(blocks):
        spread(b + 1)
    for b in range(blocks):
        load(b).wait()

    def mask_own(i, carry):
        apply_mask(RADIUS + i, 1 + i // CELLS)
        return carry

    lax.fori_loop(0, planes, mask_own, 0)

    @pl.when(jnp.logical_not(has_up))
    def _():
        phys[pl.ds(0, RADIUS)] = jnp.zeros((RADIUS, rows, columns), jnp.float32)

    @pl.when(jnp.logical_not(has_down))
    def _():
        phys[pl.ds(RADIUS + planes, RADIUS)] = jnp.zeros((RADIUS, rows, columns), jnp.float32)

    @pl.when(jnp.logical_not(has_prev))
    def _():
        yb[:, :, pl.ds(0, SUBLANES)] = jnp.zeros((layers, nx, SUBLANES, columns), jnp.float32)

    @pl.when(jnp.logical_not(has_next))
    def _():
        yb[:, :, pl.ds(SUBLANES, SUBLANES)] = jnp.zeros((layers, nx, SUBLANES, columns), jnp.float32)

    def piece(k, p, row):
        return pltpu.make_async_remote_copy(
            src_ref=zf.at[row],
            dst_ref=recv.at[k, gx],
            send_sem=send_sem.at[k, p],
            recv_sem=recv_sem.at[k, gx],
            device_id={"gx": p},
            device_id_type=MESH,
        )

    def z_step(k, carry):
        for p in range(nx):
            row = layers - 1 - k if p == 0 else p * layers + k
            part = rows // 4
            for i in range(4):
                at = pl.ds(i * part, part)
                run = phys[row + RADIUS, at]
                total = run
                for d in range(1, RADIUS + 1):
                    run = run + (phys[row + RADIUS - d, at] + phys[row + RADIUS + d, at])
                    total = total + run if d < RADIUS else total + run
                zf[row, at] = total

            @pl.when(gx != p)
            def _():
                piece(k, p, row).start()

            @pl.when(gx == p)
            def _():
                pltpu.make_async_copy(zf.at[row], recv.at[k, gx], recv_sem.at[k, gx]).start()

        return carry

    free = layers - RADIUS
    lax.fori_loop(0, free, z_step, 0)

    @pl.when(has_up)
    def _():
        mask_previous().wait_send()
        pltpu.make_async_copy(mask.at[0], masks.at[0], hmask_recv.at[0]).wait()
        spread(0)

    @pl.when(has_down)
    def _():
        mask_next().wait_send()
        pltpu.make_async_copy(mask.at[0], masks.at[blocks + 1], hmask_recv.at[1]).wait()
        spread(blocks + 1)

    def halo_step(k, carry):
        j = k - free

        @pl.when(has_up)
        def _():
            row = RADIUS - 1 - j
            pltpu.make_async_copy(density.at[0], phys.at[row], halo_recv.at[0, j]).wait()
            apply_mask(row, 0)

        @pl.when(has_down)
        def _():
            row = RADIUS + planes + j
            pltpu.make_async_copy(density.at[0], phys.at[row], halo_recv.at[1, j]).wait()
            apply_mask(row, blocks + 1)

        return z_step(k, carry)

    lax.fori_loop(free, layers, halo_step, 0)

    def y_previous(k):
        return pltpu.make_async_remote_copy(
            src_ref=recv.at[k, :, pl.ds(0, SUBLANES)],
            dst_ref=yb.at[k, :, pl.ds(SUBLANES, SUBLANES)],
            send_sem=y_send.at[k, 0],
            recv_sem=y_recv.at[k, 1],
            device_id={"gy": gy - 1},
            device_id_type=MESH,
        )

    def y_next(k):
        return pltpu.make_async_remote_copy(
            src_ref=recv.at[k, :, pl.ds(rows - SUBLANES, SUBLANES)],
            dst_ref=yb.at[k, :, pl.ds(0, SUBLANES)],
            send_sem=y_send.at[k, 1],
            recv_sem=y_recv.at[k, 0],
            device_id={"gy": gy + 1},
            device_id_type=MESH,
        )

    def x_filter(chunks, put):
        high, low = zip(*[halves(chunk) for chunk in chunks])
        none = jnp.zeros((chunks[0].shape[0], LANES), jnp.bfloat16)
        for c in range(nx):
            total = dot(high[c], w_own[...]) + dot(low[c], w_own[...])
            for part in (high, low):
                left = part[c - 1][:, columns - LANES :] if c > 0 else none
                right = part[c + 1][:, :LANES] if c < nx - 1 else none
                total = total + dot(jnp.concatenate([left, right], 1), w_edge[...])
            put(c, total)

    y_own = hat(rows, rows, 0).astype(jnp.bfloat16)
    y_edge = jnp.concatenate(
        [hat(rows, SUBLANES, -SUBLANES), hat(rows, SUBLANES, rows)], 1
    ).astype(jnp.bfloat16)

    def finish(k):
        layer = jnp.where(gx == 0, layers - 1 - k, k)
        return pltpu.make_async_copy(stage.at[k], out.at[layer], out_sem.at[k])

    def take_step(k, carry):
        for c in range(nx):
            pltpu.make_async_copy(zf.at[0], recv.at[k, c], recv_sem.at[k, c]).wait()
        pl.when(has_prev)(lambda: y_previous(k).start())
        pl.when(has_next)(lambda: y_next(k).start())

        def put_own(c, total):
            high, low = halves(total)
            at = pl.ds(c * columns, columns)
            xs[pl.ds(0, rows), at] = high
            xs[pl.ds(rows, rows), at] = low

        def put_edge(c, total):
            high, low = halves(total)
            at = pl.ds(c * columns, columns)
            xs[pl.ds(2 * rows, 2 * SUBLANES), at] = high
            xs[pl.ds(2 * rows + 2 * SUBLANES, 2 * SUBLANES), at] = low

        x_filter([recv[k, c] for c in range(nx)], put_own)

        @pl.when(has_prev)
        def _():
            y_previous(k).wait_send()
            part = yb.at[k, :, pl.ds(0, SUBLANES)]
            pltpu.make_async_copy(part, part, y_recv.at[k, 0]).wait()

        @pl.when(has_next)
        def _():
            y_next(k).wait_send()
            part = yb.at[k, :, pl.ds(SUBLANES, SUBLANES)]
            pltpu.make_async_copy(part, part, y_recv.at[k, 1]).wait()

        x_filter([yb[k, c] for c in range(nx)], put_edge)
        y_weights = jnp.concatenate([y_own, y_own], 1)
        e_weights = jnp.concatenate([y_edge, y_edge], 1)
        for c in range(nx):
            at = pl.ds(c * columns, columns)
            stage[k, :, at] = dot(y_weights, xs[pl.ds(0, 2 * rows), at]) + dot(
                e_weights, xs[pl.ds(2 * rows, 4 * SUBLANES), at]
            )
        finish(k).start()
        return carry

    lax.fori_loop(0, layers, take_step, 0)

    @pl.when(has_down)
    def _():
        for j in range(RADIUS):
            to_next(j).wait_send()

    @pl.when(has_up)
    def _():
        for j in range(RADIUS):
            to_previous(j).wait_send()

    def settle(k, carry):
        for p in range(nx):

            @pl.when(gx != p)
            def _():
                piece(k, p, 0).wait_send()

        finish(k).wait()
        return carry

    lax.fori_loop(0, layers, settle, 0)


def filtered_sums(sizes, density, mask):
    planes, rows, columns = density.shape
    nz, nx, ny = sizes
    layers = planes // nx
    blocks = mask.shape[0]
    width = nx * columns
    dma = pltpu.SemaphoreType.DMA
    return pl.pallas_call(
        functools.partial(kernel, sizes),
        out_shape=jax.ShapeDtypeStruct((layers, rows, width), jnp.float32),
        in_specs=[pl.BlockSpec(memory_space=pl.ANY)] * 2,
        out_specs=pl.BlockSpec(memory_space=pl.ANY),
        scratch_shapes=[
            pltpu.VMEM((planes + 2 * RADIUS, rows, columns), jnp.float32),
            pltpu.VMEM((blocks + 2, rows, columns), jnp.float32),
            pltpu.VMEM((blocks + 2,) + mask.shape[1:], jnp.int32),
            pltpu.VMEM((planes, rows, columns), jnp.float32),
            pltpu.VMEM((layers, nx, rows, columns), jnp.float32),
            pltpu.VMEM((layers, nx, 2 * SUBLANES, columns), jnp.float32),
            pltpu.VMEM((2 * rows + 4 * SUBLANES, width), jnp.bfloat16),
            pltpu.VMEM((layers, rows, width), jnp.float32),
            pltpu.VMEM((columns, columns), jnp.bfloat16),
            pltpu.VMEM((2 * LANES, columns), jnp.bfloat16),
            dma((blocks,)),
            dma,
            dma((2,)),
            dma((2,)),
            dma((2, RADIUS)),
            dma((2, RADIUS)),
            dma((layers, nx)),
            dma((layers, nx)),
            dma((layers, 2)),
            dma((layers, 2)),
            dma((layers,)),
        ],
        compiler_params=pltpu.CompilerParams(
            collective_id=0, has_side_effects=True, vmem_limit_bytes=48 * 1024 * 1024
        ),
    )(density, mask)


def one_side(reach):
    return reach * (RADIUS + 1) - reach * (reach + 1) // 2


def edge_sums(start, length, length_all):
    position = start + lax.iota(jnp.int32, length)
    reach_left = jnp.minimum(position, RADIUS)
    reach_right = jnp.minimum(length_all - 1 - position, RADIUS)
    return (RADIUS + 1 + one_side(reach_left) + one_side(reach_right)).astype(jnp.float32)


def body(sizes, density, mask):
    planes, rows, columns = density.shape
    nz, nx, ny = sizes
    layers = planes // nx
    summed = filtered_sums(sizes, density, mask)
    scale_x = 1.0 / edge_sums(0, columns * nx, columns * nx)
    scale_y = 1.0 / edge_sums(lax.axis_index("gy") * rows, rows, rows * ny)
    scale_z = 1.0 / edge_sums(lax.axis_index(("gz", "gx")) * layers, layers, planes * nz)
    scale = scale_z[:, None, None] * scale_y[None, :, None] * scale_x[None, None, :]
    filtered = summed * scale
    top = math.tanh(sharpness * threshold)
    bottom = top + math.tanh(sharpness * (1.0 - threshold))
    projected = (top + jnp.tanh(sharpness * (filtered - threshold))) * (1.0 / bottom)
    return (filtered, projected)


def solution(mesh):
    sizes = (mesh.shape["gz"], mesh.shape["gx"], mesh.shape["gy"])
    placed = (P("gz", "gy", "gx"), P("gz", "gy", "gx"))
    return jax.shard_map(
        functools.partial(body, sizes),
        mesh=mesh,
        in_specs=placed,
        out_specs=(P(("gz", "gx"), "gy", None), P(("gz", "gx"), "gy", None)),
        check_vma=False,
    )
```

time: 269 us -> 60.9 us (0.23)
  waiting for transfers between devices: 177 us -> 0 us
  Pallas kernels: 0 us -> 54.7 us
  local copies, waits for them, and re-layouts: 28 us -> 0.75 us
  matrix products: 25.5 us -> 0 us
  between operations: 14.2 us -> 0.67 us
  starting transfers between devices: 9.83 us -> 0 us
  other arithmetic: 14.1 us -> 4.55 us
    all_gather x1 -> x0, waiting for transfers between devices: 160 us -> none  [body(): gathered = lax.all_gather(physical, 'gx', axis=2, tiled=True)]
    pallas_call x0 -> x1, Pallas kernels: none -> 54.7 us  [filtered_sums(): pl.pallas_call(functools.partial(kernel, sizes), out_shape=jax.ShapeDtype...]
    dot_general x4 -> x0, matrix products: 25.5 us -> none  [the longest x1 8.17 us: along_first(): jnp.dot(kernel, flat, precision=highest, preferred_element_type=jnp.float32)]
    ppermute x4 -> x0, waiting for transfers between devices: 17 us -> none  [the longest x1 15.5 us: with_halo(): after = lax.ppermute(leading, axis, down)]
    ppermute x4 -> x0, starting transfers between devices: 9.8 us -> none  [the longest x1 5.63 us: with_halo(): before = lax.ppermute(last, axis, up)]
    div x1 -> x3, other arithmetic: 6.76 us -> 0.06 us  [the longest x1 0.02 us: body(): scale_y = 1.0 / edge_sums(lax.axis_index('gy') * rows, rows, rows * ny)]
    concatenate x1 -> x0, local copies, waits for them, and re-layouts: 6.27 us -> none  [with_halo(): x = jnp.concatenate([before, x, after], axis=dim)]
    unnamed x3 -> x2, local copies, waits for them, and re-layouts: 5.58 us -> 0.75 us
  transfers between devices with their start and end apart: 5 -> 0, of which waited for: 4 -> 0; matrix products, arithmetic and copies ran while one was open for 2% -> 0% of each run, Pallas kernels for 0% -> 0%
where the time goes in v1:
time: 60.9 us; the launch traced here: 60.7 us
  Pallas kernels  54.7 us (90%)
  other arithmetic  4.55 us (7%)
  local copies, waits for them, and re-layouts  0.75 us (1%)
  between operations  0.67 us (1%)
    pallas_call x1, Pallas kernels, filtered_sums(): pl.pallas_call(functools.partial(kernel, sizes), out_shape=jax.ShapeDtype...  54.7 us
    mul x1, other arithmetic, body(): (top + jnp.tanh(sharpness * (filtered - threshold))) * (1.0 / bottom)  4.42 us

profile of v1, /device:TPU:0, one launch (start us, length us, event | category | flops | bytes accessed | tf_op | source)
XLA Modules:
  0.0 60.7 jit_solution(14890390239927104669)
XLA Ops:
  0.7 0.1 broadcast_multiply_fusion
  0.8 0.0 copy-start
  0.8 0.8 %copy-done = s32[4,16,32]{2,1,0:T(8,128)S(1)} copy-done((s32[4,16,32]{2,1,0:T(8,128)S(1)}, s32[4,16,32]{2,1,0:T(8,128)}, u32[]{:S(2)}) %copy-start) | copy-done | bytes 8216
  1.5 54.7 %shard_map.41 = f32[8,128,1024]{2,1,0:T(8,128)S(1)} custom-call(f32[32,128,256]{2,1,0:T(8,128)} %density.1, s32[4,16,32]{2,1,0:T(8,128)S(1)} %copy-done), custom_call_target="tpu_custom_call" | custom-call | tf_op jit(solution)/shard_map/pallas_call | solution.py:385
  56.2 4.4 %add_multiply_fusion = (f32[8,128,1024]{2,1,0:T(8,128)}, f32[8,128,1024]{2,1,0:T(8,128)}) fusion(f32[8,128,1024]{2,1,0:T(8,128)S(1)} %shard_map.41, f32[1024]{0:T(1024)S(1)} %fusion.10, f32[8,128]{1,0:T(8,128)S(1)} %broadcast_multiply_fusion), kind=kLoop, calls=%fused_computation | loop fusion | flops 6291456 | bytes 12591104 | tf_op jit(solution)/shard_map/mul | solution.py:442
  (3 shorter events, 0.1 us)
Async XLA Ops:
  0.8 0.8 %copy-start = (s32[4,16,32]{2,1,0:T(8,128)S(1)}, s32[4,16,32]{2,1,0:T(8,128)}, u32[]{:S(2)}) copy-start(s32[4,16,32]{2,1,0:T(8,128)} %mask.1) | copy-start | bytes 24580

commit v2 on v1

v2 whole, which is shorter than its diff:
```python
import functools
import math

import jax
import jax.numpy as jnp
from jax import lax
from jax.experimental import pallas as pl
from jax.experimental.pallas import tpu as pltpu
from jax.sharding import PartitionSpec as P

RADIUS = 6
CELLS = 8
LANES = 128
SUBLANES = 8

sharpness = 8.0
threshold = 0.5
MESH = pl.DeviceIdType.MESH


def hat(rows, cols, offset):
    row = lax.broadcasted_iota(jnp.int32, (rows, cols), 0)
    col = lax.broadcasted_iota(jnp.int32, (rows, cols), 1)
    return jnp.maximum(RADIUS + 1 - jnp.abs(col + offset - row), 0).astype(jnp.float32)


def halves(values):
    high = values.astype(jnp.bfloat16)
    low = (values - high.astype(jnp.float32)).astype(jnp.bfloat16)
    return high, low


def projection(filtered):
    top = math.tanh(sharpness * threshold)
    bottom = top + math.tanh(sharpness * (1.0 - threshold))
    return (top + jnp.tanh(sharpness * (filtered - threshold))) * (1.0 / bottom)


def one_side(reach):
    return reach * (RADIUS + 1) - reach * (reach + 1) // 2


def dot(a, b):
    return jnp.dot(a, b, preferred_element_type=jnp.float32)


def x_filter(chunks, w_own, w_edge, xs, first):
    size, columns = chunks[0].shape
    high, low = zip(*[halves(chunk) for chunk in chunks])
    none = jnp.zeros((size, LANES), jnp.bfloat16)
    for c in range(len(chunks)):
        total = dot(high[c], w_own[...]) + dot(low[c], w_own[...])
        for part in (high, low):
            left = part[c - 1][:, columns - LANES :] if c > 0 else none
            right = part[c + 1][:, :LANES] if c < len(chunks) - 1 else none
            total = total + dot(jnp.concatenate([left, right], 1), w_edge[...])
        at = pl.ds(c * columns, columns)
        xs[pl.ds(first, size), at], xs[pl.ds(first + size, size), at] = halves(total)


def y_filter(xs, scale, scale_z, columns, put):
    rows, width = scale.shape
    own = hat(rows, rows, 0).astype(jnp.bfloat16)
    edge = jnp.concatenate([hat(rows, SUBLANES, -SUBLANES), hat(rows, SUBLANES, rows)], 1)
    edge = edge.astype(jnp.bfloat16)
    own = jnp.concatenate([own, own], 1)
    edge = jnp.concatenate([edge, edge], 1)
    for c in range(width // columns):
        at = pl.ds(c * columns, columns)
        summed = dot(own, xs[pl.ds(0, 2 * rows), at])
        summed = summed + dot(edge, xs[pl.ds(2 * rows, 4 * SUBLANES), at])
        put(at, summed * (scale[:, at] * scale_z))


def inverse_count(position, length):
    left = one_side(jnp.minimum(position, RADIUS))
    right = one_side(jnp.minimum(length - 1 - position, RADIUS))
    return 1.0 / (RADIUS + 1 + left + right).astype(jnp.float32)


def layer_of(k, layers):
    return jnp.where(lax.axis_index("gx") == 0, layers - 1 - k, k)


def scale_along_z(sizes, k, layers, columns):
    nz, nx, ny = sizes
    level = (lax.axis_index("gz") * nx + lax.axis_index("gx")) * layers + layer_of(k, layers)
    level = jnp.full((SUBLANES, columns), level, jnp.int32)
    return inverse_count(level, nz * nx * layers)[0:1]


def kernel(
    sizes,
    density,
    mask,
    fstage,
    pstage,
    lrecv,
    lyb,
    scale,
    w_own,
    w_edge,
    phys,
    codes,
    masks,
    zf,
    recv,
    yb,
    xs,
    load_sem,
    mask_sem,
    hmask_send,
    hmask_recv,
    halo_send,
    halo_recv,
    send_sem,
    recv_sem,
    y_send,
    y_recv,
    e_send,
    e_recv,
):
    nz, nx, ny = sizes
    planes, rows, columns = density.shape
    blocks = mask.shape[0]
    layers = planes // nx
    gz, gx, gy = lax.axis_index("gz"), lax.axis_index("gx"), lax.axis_index("gy")
    has_up, has_down = gz > 0, gz < nz - 1
    has_prev, has_next = gy > 0, gy < ny - 1

    def load(b):
        part = pl.ds(b * CELLS, CELLS)
        return pltpu.make_async_copy(
            density.at[part], phys.at[pl.ds(RADIUS + b * CELLS, CELLS)], load_sem.at[b]
        )

    mask_copy = pltpu.make_async_copy(mask, masks.at[pl.ds(1, blocks)], mask_sem)
    mask_copy.start()
    for b in range(blocks):
        load(b).start()

    barrier = pltpu.get_barrier_semaphore()

    def greet(**where):
        pl.semaphore_signal(barrier, inc=1, device_id=where, device_id_type=MESH)

    pl.when(has_up)(lambda: greet(gz=gz - 1))
    pl.when(has_down)(lambda: greet(gz=gz + 1))
    pl.when(has_prev)(lambda: greet(gy=gy - 1))
    pl.when(has_next)(lambda: greet(gy=gy + 1))
    for step in range(1, nx):
        greet(gx=lax.rem(gx + step, nx))

    def to_next(j):
        return pltpu.make_async_remote_copy(
            src_ref=density.at[planes - 1 - j],
            dst_ref=phys.at[RADIUS - 1 - j],
            send_sem=halo_send.at[0, j],
            recv_sem=halo_recv.at[0, j],
            device_id={"gz": gz + 1},
            device_id_type=MESH,
        )

    def to_previous(j):
        return pltpu.make_async_remote_copy(
            src_ref=density.at[j],
            dst_ref=phys.at[RADIUS + planes + j],
            send_sem=halo_send.at[1, j],
            recv_sem=halo_recv.at[1, j],
            device_id={"gz": gz - 1},
            device_id_type=MESH,
        )

    def mask_next():
        return pltpu.make_async_remote_copy(
            src_ref=mask.at[blocks - 1],
            dst_ref=masks.at[0],
            send_sem=hmask_send.at[0],
            recv_sem=hmask_recv.at[0],
            device_id={"gz": gz + 1},
            device_id_type=MESH,
        )

    def mask_previous():
        return pltpu.make_async_remote_copy(
            src_ref=mask.at[0],
            dst_ref=masks.at[blocks + 1],
            send_sem=hmask_send.at[1],
            recv_sem=hmask_recv.at[1],
            device_id={"gz": gz - 1},
            device_id_type=MESH,
        )

    def spread(b):
        small = masks[b].astype(jnp.float32).astype(jnp.bfloat16)
        mrows, mcols = small.shape
        r = lax.broadcasted_iota(jnp.int32, (rows, mrows), 0) // CELLS
        m = lax.broadcasted_iota(jnp.int32, (rows, mrows), 1)
        tall = dot(jnp.where(r == m, 1.0, 0.0).astype(jnp.bfloat16), small)
        c = lax.broadcasted_iota(jnp.int32, (mcols, columns), 1) // CELLS
        n = lax.broadcasted_iota(jnp.int32, (mcols, columns), 0)
        wide = jnp.where(c == n, 1.0, 0.0).astype(jnp.bfloat16)
        codes[b] = dot(tall.astype(jnp.bfloat16), wide)

    def apply_mask(row, b):
        code = codes[b]
        phys[row] = jnp.where(code < 0.5, 0.0, jnp.where(code < 1.5, 1.0, phys[row]))

    def piece(k, p, row):
        return pltpu.make_async_remote_copy(
            src_ref=zf.at[row],
            dst_ref=recv.at[k, gx],
            send_sem=send_sem.at[k, p],
            recv_sem=recv_sem.at[k, gx],
            device_id={"gx": p},
            device_id_type=MESH,
        )

    edges = (pl.ds(0, SUBLANES), pl.ds(rows - SUBLANES, SUBLANES))
    inside = pl.ds(SUBLANES, rows - 2 * SUBLANES)

    def edge_piece(side, p, row):
        return pltpu.make_async_remote_copy(
            src_ref=zf.at[row, edges[side]],
            dst_ref=lrecv.at[gx, edges[side]],
            send_sem=e_send.at[side, p],
            recv_sem=e_recv.at[side, gx],
            device_id={"gx": p},
            device_id_type=MESH,
        )

    def inner_piece(p, row):
        return pltpu.make_async_remote_copy(
            src_ref=zf.at[row, inside],
            dst_ref=lrecv.at[gx, inside],
            send_sem=send_sem.at[layers - 1, p],
            recv_sem=recv_sem.at[layers - 1, gx],
            device_id={"gx": p},
            device_id_type=MESH,
        )

    def row_of(k, p):
        return layers - 1 - k if p == 0 else p * layers + k

    def z_filter(row):
        part = rows // 4
        for i in range(4):
            at = pl.ds(i * part, part)
            run = phys[row + RADIUS, at]
            total = run
            for d in range(1, RADIUS + 1):
                run = run + (phys[row + RADIUS - d, at] + phys[row + RADIUS + d, at])
                total = total + run
            zf[row, at] = total

    def z_send(k, p):
        row = row_of(k, p)
        z_filter(row)

        @pl.when(gx != p)
        def _():
            piece(k, p, row).start()

        @pl.when(gx == p)
        def _():
            pltpu.make_async_copy(zf.at[row], recv.at[k, gx], recv_sem.at[k, gx]).start()

    def z_step(k, carry):
        for p in range(nx):
            z_send(k, p)
        return carry

    def mask_block(b):
        spread(b + 1)
        load(b).wait()

        def one(i, carry):
            apply_mask(RADIUS + b * CELLS + i, b + 1)
            return carry

        lax.fori_loop(0, CELLS, one, 0)

    mask_copy.wait()
    ready = 0
    for p in range(nx):
        need = min(blocks, (row_of(0, p) + RADIUS) // CELLS + 1)
        for b in range(ready, need):
            mask_block(b)
        if p == 0:
            count = nx - 1
            for there in (has_up, has_down, has_prev, has_next):
                count = count + there.astype(jnp.int32)
            pl.semaphore_wait(barrier, count)
        ready = max(ready, need)
        z_send(0, p)
    for b in range(ready, blocks):
        mask_block(b)

    @pl.when(has_down)
    def _():
        mask_next().start()
        for j in range(RADIUS):
            to_next(j).start()

    @pl.when(has_up)
    def _():
        mask_previous().start()
        for j in range(RADIUS):
            to_previous(j).start()

    @pl.when(jnp.logical_not(has_up))
    def _():
        phys[pl.ds(0, RADIUS)] = jnp.zeros((RADIUS, rows, columns), jnp.float32)

    @pl.when(jnp.logical_not(has_down))
    def _():
        phys[pl.ds(RADIUS + planes, RADIUS)] = jnp.zeros((RADIUS, rows, columns), jnp.float32)

    @pl.when(jnp.logical_not(has_prev))
    def _():
        lyb[:, pl.ds(0, SUBLANES)] = jnp.zeros((nx, SUBLANES, columns), jnp.float32)
        yb[:, :, pl.ds(0, SUBLANES)] = jnp.zeros((layers - 1, nx, SUBLANES, columns), jnp.float32)

    @pl.when(jnp.logical_not(has_next))
    def _():
        lyb[:, pl.ds(SUBLANES, SUBLANES)] = jnp.zeros((nx, SUBLANES, columns), jnp.float32)
        yb[:, :, pl.ds(SUBLANES, SUBLANES)] = jnp.zeros((layers - 1, nx, SUBLANES, columns), jnp.float32)

    free = layers - RADIUS
    lax.fori_loop(1, free, z_step, 0)

    w_own[...] = hat(columns, columns, 0).astype(jnp.bfloat16)
    w_edge[pl.ds(0, LANES)] = hat(LANES, columns, LANES).astype(jnp.bfloat16)
    w_edge[pl.ds(LANES, LANES)] = hat(LANES, columns, -columns).astype(jnp.bfloat16)

    width = nx * columns
    scale_y = inverse_count(
        gy * rows + lax.broadcasted_iota(jnp.int32, (rows, LANES), 0), rows * ny
    )
    for c in range(0, width, LANES):
        lane = c + lax.broadcasted_iota(jnp.int32, (SUBLANES, LANES), 1)
        scale_x = inverse_count(lane, width)
        scale[:, pl.ds(c, LANES)] = scale_y * scale_x[0:1]

    @pl.when(has_up)
    def _():
        mask_previous().wait_send()
        pltpu.make_async_copy(mask.at[0], masks.at[0], hmask_recv.at[0]).wait()
        spread(0)

    @pl.when(has_down)
    def _():
        mask_next().wait_send()
        pltpu.make_async_copy(mask.at[0], masks.at[blocks + 1], hmask_recv.at[1]).wait()
        spread(blocks + 1)

    def take_halo(k):
        j = k - free

        @pl.when(has_up)
        def _():
            row = RADIUS - 1 - j
            pltpu.make_async_copy(density.at[0], phys.at[row], halo_recv.at[0, j]).wait()
            apply_mask(row, 0)

        @pl.when(has_down)
        def _():
            row = RADIUS + planes + j
            pltpu.make_async_copy(density.at[0], phys.at[row], halo_recv.at[1, j]).wait()
            apply_mask(row, blocks + 1)

    def halo_step(k, carry):
        take_halo(k)
        return z_step(k, carry)

    final = layers - 1
    lax.fori_loop(free, final, halo_step, 0)

    take_halo(final)
    for p in range(nx):
        row = row_of(final, p)
        z_filter(row)

        @pl.when(gx != p)
        def _():
            edge_piece(0, p, row).start()
            edge_piece(1, p, row).start()

        @pl.when(gx == p)
        def _():
            for side in range(2):
                pltpu.make_async_copy(
                    zf.at[row, edges[side]], lrecv.at[gx, edges[side]], e_recv.at[side, gx]
                ).start()
            pltpu.make_async_copy(
                zf.at[row, inside], lrecv.at[gx, inside], recv_sem.at[final, gx]
            ).start()

    for p in range(nx):

        @pl.when(gx != p)
        def _():
            inner_piece(p, row_of(final, p)).start()

    def y_previous(k):
        return pltpu.make_async_remote_copy(
            src_ref=recv.at[k, :, pl.ds(0, SUBLANES)],
            dst_ref=yb.at[k, :, pl.ds(SUBLANES, SUBLANES)],
            send_sem=y_send.at[k, 0],
            recv_sem=y_recv.at[k, 1],
            device_id={"gy": gy - 1},
            device_id_type=MESH,
        )

    def y_next(k):
        return pltpu.make_async_remote_copy(
            src_ref=recv.at[k, :, pl.ds(rows - SUBLANES, SUBLANES)],
            dst_ref=yb.at[k, :, pl.ds(0, SUBLANES)],
            send_sem=y_send.at[k, 1],
            recv_sem=y_recv.at[k, 0],
            device_id={"gy": gy + 1},
            device_id_type=MESH,
        )

    def last_previous():
        return pltpu.make_async_remote_copy(
            src_ref=lrecv.at[:, pl.ds(0, SUBLANES)],
            dst_ref=lyb.at[:, pl.ds(SUBLANES, SUBLANES)],
            send_sem=y_send.at[final, 0],
            recv_sem=y_recv.at[final, 1],
            device_id={"gy": gy - 1},
            device_id_type=MESH,
        )

    def last_next():
        return pltpu.make_async_remote_copy(
            src_ref=lrecv.at[:, pl.ds(rows - SUBLANES, SUBLANES)],
            dst_ref=lyb.at[:, pl.ds(0, SUBLANES)],
            send_sem=y_send.at[final, 1],
            recv_sem=y_recv.at[final, 0],
            device_id={"gy": gy + 1},
            device_id_type=MESH,
        )

    def send_edges(k):
        pl.when(has_prev)(lambda: y_previous(k).start())
        pl.when(has_next)(lambda: y_next(k).start())

    def take_edges(k):
        @pl.when(has_prev)
        def _():
            y_previous(k).wait_send()
            part = yb.at[k, :, pl.ds(0, SUBLANES)]
            pltpu.make_async_copy(part, part, y_recv.at[k, 0]).wait()

        @pl.when(has_next)
        def _():
            y_next(k).wait_send()
            part = yb.at[k, :, pl.ds(SUBLANES, SUBLANES)]
            pltpu.make_async_copy(part, part, y_recv.at[k, 1]).wait()

    def take_step(k, carry):
        for c in range(nx):
            pltpu.make_async_copy(zf.at[0], recv.at[k, c], recv_sem.at[k, c]).wait()
        send_edges(k)
        x_filter([recv[k, c] for c in range(nx)], w_own, w_edge, xs, 0)
        take_edges(k)
        x_filter([yb[k, c] for c in range(nx)], w_own, w_edge, xs, 2 * rows)

        def put(at, value):
            fstage[k, :, at] = value
            pstage[k, :, at] = projection(value)

        y_filter(xs, scale, scale_along_z(sizes, k, layers, columns), columns, put)
        return carry

    lax.fori_loop(0, final, take_step, 0)

    for c in range(nx):
        for side in range(2):
            part = lrecv.at[c, edges[side]]
            pltpu.make_async_copy(part, part, e_recv.at[side, c]).wait()
    pl.when(has_prev)(lambda: last_previous().start())
    pl.when(has_next)(lambda: last_next().start())

    @pl.when(has_down)
    def _():
        for j in range(RADIUS):
            to_next(j).wait_send()

    @pl.when(has_up)
    def _():
        for j in range(RADIUS):
            to_previous(j).wait_send()

    def settle(k, carry):
        for p in range(nx):

            @pl.when(gx != p)
            def _():
                piece(k, p, 0).wait_send()

        return carry

    lax.fori_loop(0, final, settle, 0)
    for p in range(nx):

        @pl.when(gx != p)
        def _():
            edge_piece(0, p, 0).wait_send()
            edge_piece(1, p, 0).wait_send()
            inner_piece(p, 0).wait_send()

    @pl.when(has_prev)
    def _():
        last_previous().wait_send()
        part = lyb.at[:, pl.ds(0, SUBLANES)]
        pltpu.make_async_copy(part, part, y_recv.at[final, 0]).wait()

    @pl.when(has_next)
    def _():
        last_next().wait_send()
        part = lyb.at[:, pl.ds(SUBLANES, SUBLANES)]
        pltpu.make_async_copy(part, part, y_recv.at[final, 1]).wait()

    for c in range(nx):
        part = lrecv.at[c, inside]
        pltpu.make_async_copy(part, part, recv_sem.at[final, c]).wait()


def closing(sizes, fstage, pstage, lrecv, lyb, scale, w_own, w_edge, filt, proj, xs, flast, plast, sems, last_sems):
    final = fstage.shape[0]
    nx, rows, columns = lrecv.shape
    layers = final + 1

    def finished(k):
        at = layer_of(k, layers)
        return (
            pltpu.make_async_copy(fstage.at[k], filt.at[at], sems.at[0, k]),
            pltpu.make_async_copy(pstage.at[k], proj.at[at], sems.at[1, k]),
        )

    for k in range(final):
        for copy in finished(k):
            copy.start()
    x_filter([lrecv[c] for c in range(nx)], w_own, w_edge, xs, 0)
    x_filter([lyb[c] for c in range(nx)], w_own, w_edge, xs, 2 * rows)

    def put(at, value):
        flast[:, at] = value
        plast[:, at] = projection(value)

    y_filter(xs, scale, scale_along_z(sizes, final, layers, columns), columns, put)
    at = layer_of(final, layers)
    ends = (
        pltpu.make_async_copy(flast, filt.at[at], last_sems.at[0]),
        pltpu.make_async_copy(plast, proj.at[at], last_sems.at[1]),
    )
    for copy in ends:
        copy.start()
    for k in range(final):
        for copy in finished(k):
            copy.wait()
    for copy in ends:
        copy.wait()


def body(sizes, density, mask):
    planes, rows, columns = density.shape
    nz, nx, ny = sizes
    layers = planes // nx
    final = layers - 1
    blocks = mask.shape[0]
    width = nx * columns
    dma = pltpu.SemaphoreType.DMA
    f32, bf16 = jnp.float32, jnp.bfloat16
    shape = jax.ShapeDtypeStruct
    carried = (
        shape((final, rows, width), f32),
        shape((final, rows, width), f32),
        shape((nx, rows, columns), f32),
        shape((nx, 2 * SUBLANES, columns), f32),
        shape((rows, width), f32),
        shape((columns, columns), bf16),
        shape((2 * LANES, columns), bf16),
    )
    xs = pltpu.VMEM((2 * rows + 4 * SUBLANES, width), bf16)
    held = pl.pallas_call(
        functools.partial(kernel, sizes),
        out_shape=carried,
        in_specs=[pl.BlockSpec(memory_space=pl.ANY)] * 2,
        out_specs=(pl.BlockSpec(memory_space=pltpu.VMEM),) * len(carried),
        scratch_shapes=[
            pltpu.VMEM((planes + 2 * RADIUS, rows, columns), f32),
            pltpu.VMEM((blocks + 2, rows, columns), f32),
            pltpu.VMEM((blocks + 2,) + mask.shape[1:], jnp.int32),
            pltpu.VMEM((planes, rows, columns), f32),
            pltpu.VMEM((final, nx, rows, columns), f32),
            pltpu.VMEM((final, nx, 2 * SUBLANES, columns), f32),
            xs,
            dma((blocks,)),
            dma,
            dma((2,)),
            dma((2,)),
            dma((2, RADIUS)),
            dma((2, RADIUS)),
            dma((layers, nx)),
            dma((layers, nx)),
            dma((layers, 2)),
            dma((layers, 2)),
            dma((2, nx)),
            dma((2, nx)),
        ],
        compiler_params=pltpu.CompilerParams(
            collective_id=0, has_side_effects=True, vmem_limit_bytes=44 * 1024 * 1024
        ),
    )(density, mask)
    return pl.pallas_call(
        functools.partial(closing, sizes),
        out_shape=(shape((layers, rows, width), f32),) * 2,
        in_specs=[pl.BlockSpec(memory_space=pltpu.VMEM)] * len(carried),
        out_specs=(pl.BlockSpec(memory_space=pl.ANY),) * 2,
        scratch_shapes=[
            xs,
            pltpu.VMEM((rows, width), f32),
            pltpu.VMEM((rows, width), f32),
            dma((2, final)),
            dma((2,)),
        ],
        compiler_params=pltpu.CompilerParams(vmem_limit_bytes=16 * 1024 * 1024),
    )(*held)


def solution(mesh):
    sizes = (mesh.shape["gz"], mesh.shape["gx"], mesh.shape["gy"])
    placed = (P("gz", "gy", "gx"), P("gz", "gy", "gx"))
    return jax.shard_map(
        functools.partial(body, sizes),
        mesh=mesh,
        in_specs=placed,
        out_specs=(P(("gz", "gx"), "gy", None), P(("gz", "gx"), "gy", None)),
        check_vma=False,
    )
```

time: 60.9 us -> 57.4 us (0.943)
  other arithmetic: 4.55 us -> 0 us
  Pallas kernels: 54.7 us -> 55.8 us
    mul x2 -> x0, other arithmetic: 4.49 us -> none  [the longest x1 4.42 us: body(): (top + jnp.tanh(sharpness * (filtered - threshold))) * (1.0 / bottom)]
    pallas_call x1 -> x2, Pallas kernels: 54.7 us -> 55.8 us  [the longest x1 51.9 us: body(): pl.pallas_call(functools.partial(kernel, sizes), out_shape=carried, in_sp...]
where the time goes in v2:
time: 57.4 us; the launch traced here: 57.2 us
  Pallas kernels  55.8 us (97%)
  local copies, waits for them, and re-layouts  0.75 us (1%)
  between operations  0.65 us (1%)
    pallas_call x1, Pallas kernels, body(): pl.pallas_call(functools.partial(kernel, sizes), out_shape=carried, in_sp...  51.9 us
    pallas_call x1, Pallas kernels, body(): pl.pallas_call(functools.partial(closing, sizes), out_shape=(shape((layer...  3.93 us

profile of v2, /device:TPU:0, one launch (start us, length us, event | category | flops | bytes accessed | tf_op | source)
XLA Modules:
  0.0 57.2 jit_solution(14786985555721508451)
XLA Ops:
  0.6 0.0 copy-start
  0.6 0.7 %copy-done = s32[4,16,32]{2,1,0:T(8,128)S(1)} copy-done((s32[4,16,32]{2,1,0:T(8,128)S(1)}, s32[4,16,32]{2,1,0:T(8,128)}, u32[]{:S(2)}) %copy-start) | copy-done | bytes 8216
  1.4 51.9 %shard_map.41 = (f32[7,128,1024]{2,1,0:T(8,128)S(1)}, f32[7,128,1024]{2,1,0:T(8,128)S(1)}, f32[4,128,256]{2,1,0:T(8,128)S(1)}, f32[4,16,256]{2,1,0:T(8,128)S(1)}...) custom-call(f32[32,128,256]{2,1,0:T(8,128)} %density.1, s32[4,16,32]{2,1,0:T(8,128)S(1)} %copy-done), custom_call_target="tpu_custom_call" | custom-call | tf_op jit(solution)/shard_map/pallas_call | solution.py:588
  53.3 3.9 %shard_map.42 = (f32[8,128,1024]{2,1,0:T(8,128)}, f32[8,128,1024]{2,1,0:T(8,128)}) custom-call(f32[7,128,1024]{2,1,0:T(8,128)S(1)} %get-tuple-element.9.fstage, f32[7,128,1024]{2,1,0:T(8,128)S(1)} %get-tuple-element.10.pstage, f32[4,128,256]{2,1,0:T(8,128)S(1)} %get-tuple-element.11.lrecv, f32[4,16,256]{2,1,0:T(8,128)S(1)} %get-tuple-element.12.lyb, ...), custom_call_target="tpu_custom_call" | custom-call | tf_op jit(solution)/shard_map/pallas_call | solution.py:618
Async XLA Ops:
  0.6 0.8 %copy-start = (s32[4,16,32]{2,1,0:T(8,128)S(1)}, s32[4,16,32]{2,1,0:T(8,128)}, u32[]{:S(2)}) copy-start(s32[4,16,32]{2,1,0:T(8,128)} %mask.1) | copy-start | bytes 24580

commit v3 on v2

--- a/solution.py
+++ b/solution.py
@@ -546,23 +546,29 @@
     x_filter([lrecv[c] for c in range(nx)], w_own, w_edge, xs, 0)
     x_filter([lyb[c] for c in range(nx)], w_own, w_edge, xs, 2 * rows)
 
+    level = layer_of(final, layers)
+
+    def ends(at):
+        c = at.start // columns
+        return (
+            pltpu.make_async_copy(flast.at[:, at], filt.at[level, :, at], last_sems.at[0, c]),
+            pltpu.make_async_copy(plast.at[:, at], proj.at[level, :, at], last_sems.at[1, c]),
+        )
+
     def put(at, value):
         flast[:, at] = value
+        first, second = ends(at)
+        first.start()
         plast[:, at] = projection(value)
+        second.start()
 
     y_filter(xs, scale, scale_along_z(sizes, final, layers, columns), columns, put)
-    at = layer_of(final, layers)
-    ends = (
-        pltpu.make_async_copy(flast, filt.at[at], last_sems.at[0]),
-        pltpu.make_async_copy(plast, proj.at[at], last_sems.at[1]),
-    )
-    for copy in ends:
-        copy.start()
     for k in range(final):
         for copy in finished(k):
             copy.wait()
-    for copy in ends:
-        copy.wait()
+    for c in range(nx):
+        for copy in ends(pl.ds(c * columns, columns)):
+            copy.wait()
 
 
 def body(sizes, density, mask):
@@ -625,7 +631,7 @@
             pltpu.VMEM((rows, width), f32),
             pltpu.VMEM((rows, width), f32),
             dma((2, final)),
-            dma((2,)),
+            dma((2, nx)),
         ],
         compiler_params=pltpu.CompilerParams(vmem_limit_bytes=16 * 1024 * 1024),
     )(*held)

time: 57.4 us -> 57.4 us (level)
  no operation moved by 1% of the time
where the time goes in v3:
time: 57.4 us; the launch traced here: 57.2 us
  Pallas kernels  55.8 us (97%)
  local copies, waits for them, and re-layouts  0.75 us (1%)
  between operations  0.65 us (1%)
    pallas_call x1, Pallas kernels, body(): pl.pallas_call(functools.partial(kernel, sizes), out_shape=carried, in_sp...  51.9 us
    pallas_call x1, Pallas kernels, body(): pl.pallas_call(functools.partial(closing, sizes), out_shape=(shape((layer...  3.97 us

profile of v3, /device:TPU:0, one launch (start us, length us, event | category | flops | bytes accessed | tf_op | source)
XLA Modules:
  0.0 57.2 jit_solution(7679014555221441269)
XLA Ops:
  0.6 0.0 copy-start
  0.6 0.7 %copy-done = s32[4,16,32]{2,1,0:T(8,128)S(1)} copy-done((s32[4,16,32]{2,1,0:T(8,128)S(1)}, s32[4,16,32]{2,1,0:T(8,128)}, u32[]{:S(2)}) %copy-start) | copy-done | bytes 8216
  1.4 51.9 %shard_map.41 = (f32[7,128,1024]{2,1,0:T(8,128)S(1)}, f32[7,128,1024]{2,1,0:T(8,128)S(1)}, f32[4,128,256]{2,1,0:T(8,128)S(1)}, f32[4,16,256]{2,1,0:T(8,128)S(1)}...) custom-call(f32[32,128,256]{2,1,0:T(8,128)} %density.1, s32[4,16,32]{2,1,0:T(8,128)S(1)} %copy-done), custom_call_target="tpu_custom_call" | custom-call | tf_op jit(solution)/shard_map/pallas_call | solution.py:594
  53.3 4.0 %shard_map.42 = (f32[8,128,1024]{2,1,0:T(8,128)}, f32[8,128,1024]{2,1,0:T(8,128)}) custom-call(f32[7,128,1024]{2,1,0:T(8,128)S(1)} %get-tuple-element.9.fstage, f32[7,128,1024]{2,1,0:T(8,128)S(1)} %get-tuple-element.10.pstage, f32[4,128,256]{2,1,0:T(8,128)S(1)} %get-tuple-element.11.lrecv, f32[4,16,256]{2,1,0:T(8,128)S(1)} %get-tuple-element.12.lyb, ...), custom_call_target="tpu_custom_call" | custom-call | tf_op jit(solution)/shard_map/pallas_call | solution.py:624
Async XLA Ops:
  0.6 0.8 %copy-start = (s32[4,16,32]{2,1,0:T(8,128)S(1)}, s32[4,16,32]{2,1,0:T(8,128)}, u32[]{:S(2)}) copy-start(s32[4,16,32]{2,1,0:T(8,128)} %mask.1) | copy-start | bytes 24580

commit v4 on v3

--- a/solution.py
+++ b/solution.py
@@ -271,7 +271,6 @@
         return carry
 
     def mask_block(b):
-        spread(b + 1)
         load(b).wait()
 
         def one(i, carry):
@@ -281,6 +280,8 @@
         lax.fori_loop(0, CELLS, one, 0)
 
     mask_copy.wait()
+    for b in range(blocks):
+        spread(b + 1)
     ready = 0
     for p in range(nx):
         need = min(blocks, (row_of(0, p) + RADIUS) // CELLS + 1)
@@ -396,9 +397,16 @@
                 zf.at[row, inside], lrecv.at[gx, inside], recv_sem.at[final, gx]
             ).start()
 
+    mirror = nx - 1 - gx
+
+    @pl.when(gx != mirror)
+    def _():
+        row = jnp.where(mirror == 0, layers - 1 - final, mirror * layers + final)
+        inner_piece(mirror, row).start()
+
     for p in range(nx):
 
-        @pl.when(gx != p)
+        @pl.when(jnp.logical_and(gx != p, mirror != p))
         def _():
             inner_piece(p, row_of(final, p)).start()
 

time: 57.4 us -> 57.6 us (level)
  no operation moved by 1% of the time
where the time goes in v4:
time: 57.6 us; the launch traced here: 57.4 us
  Pallas kernels  56 us (97%)
  local copies, waits for them, and re-layouts  0.75 us (1%)
  between operations  0.65 us (1%)
    pallas_call x1, Pallas kernels, body(): pl.pallas_call(functools.partial(kernel, sizes), out_shape=carried, in_sp...  52 us
    pallas_call x1, Pallas kernels, body(): pl.pallas_call(functools.partial(closing, sizes), out_shape=(shape((layer...  3.97 us

profile of v4, /device:TPU:0, one launch (start us, length us, event | category | flops | bytes accessed | tf_op | source)
XLA Modules:
  0.0 57.4 jit_solution(6644786990742715563)
XLA Ops:
  0.6 0.0 copy-start
  0.6 0.7 %copy-done = s32[4,16,32]{2,1,0:T(8,128)S(1)} copy-done((s32[4,16,32]{2,1,0:T(8,128)S(1)}, s32[4,16,32]{2,1,0:T(8,128)}, u32[]{:S(2)}) %copy-start) | copy-done | bytes 8216
  1.4 52.0 %shard_map.41 = (f32[7,128,1024]{2,1,0:T(8,128)S(1)}, f32[7,128,1024]{2,1,0:T(8,128)S(1)}, f32[4,128,256]{2,1,0:T(8,128)S(1)}, f32[4,16,256]{2,1,0:T(8,128)S(1)}...) custom-call(f32[32,128,256]{2,1,0:T(8,128)} %density.1, s32[4,16,32]{2,1,0:T(8,128)S(1)} %copy-done), custom_call_target="tpu_custom_call" | custom-call | tf_op jit(solution)/shard_map/pallas_call | solution.py:602
  53.4 4.0 %shard_map.42 = (f32[8,128,1024]{2,1,0:T(8,128)}, f32[8,128,1024]{2,1,0:T(8,128)}) custom-call(f32[7,128,1024]{2,1,0:T(8,128)S(1)} %get-tuple-element.9.fstage, f32[7,128,1024]{2,1,0:T(8,128)S(1)} %get-tuple-element.10.pstage, f32[4,128,256]{2,1,0:T(8,128)S(1)} %get-tuple-element.11.lrecv, f32[4,16,256]{2,1,0:T(8,128)S(1)} %get-tuple-element.12.lyb, ...), custom_call_target="tpu_custom_call" | custom-call | tf_op jit(solution)/shard_map/pallas_call | solution.py:632
Async XLA Ops:
  0.6 0.8 %copy-start = (s32[4,16,32]{2,1,0:T(8,128)S(1)}, s32[4,16,32]{2,1,0:T(8,128)}, u32[]{:S(2)}) copy-start(s32[4,16,32]{2,1,0:T(8,128)} %mask.1) | copy-start | bytes 24580

commit v5 on v2

--- a/solution.py
+++ b/solution.py
@@ -614,7 +614,7 @@
         compiler_params=pltpu.CompilerParams(
             collective_id=0, has_side_effects=True, vmem_limit_bytes=44 * 1024 * 1024
         ),
-    )(density, mask)
+    )(density, jnp.minimum(mask, 2))
     return pl.pallas_call(
         functools.partial(closing, sizes),
         out_shape=(shape((layers, rows, width), f32),) * 2,

time: 57.4 us -> 57.4 us (level)
  other arithmetic: 0 us -> 0.76 us
  local copies, waits for them, and re-layouts: 0.75 us -> 0 us
    min x0 -> x1, other arithmetic: none -> 0.76 us  [body(): jnp.minimum(mask, 2)]
    unnamed x2 -> x0, local copies, waits for them, and re-layouts: 0.75 us -> none
where the time goes in v5:
time: 57.4 us; the launch traced here: 57.2 us
  Pallas kernels  55.8 us (97%)
  other arithmetic  0.76 us (1%)
  between operations  0.64 us (1%)
    pallas_call x1, Pallas kernels, body(): pl.pallas_call(functools.partial(kernel, sizes), out_shape=carried, in_sp...  51.9 us
    pallas_call x1, Pallas kernels, body(): pl.pallas_call(functools.partial(closing, sizes), out_shape=(shape((layer...  3.94 us

profile of v5, /device:TPU:0, one launch (start us, length us, event | category | flops | bytes accessed | tf_op | source)
XLA Modules:
  0.0 57.2 jit_solution(8863679031005705301)
XLA Ops:
  0.6 0.8 %broadcast_minimum_fusion.mask = s32[4,16,32]{2,1,0:T(8,128)S(1)} fusion(s32[4,16,32]{2,1,0:T(8,128)} %param.3), kind=kLoop, calls=%fused_computation | loop fusion | flops 2048 | bytes 16384 | tf_op jit(solution)/shard_map/min | solution.py:617
  1.4 51.9 %shard_map.41 = (f32[7,128,1024]{2,1,0:T(8,128)S(1)}, f32[7,128,1024]{2,1,0:T(8,128)S(1)}, f32[4,128,256]{2,1,0:T(8,128)S(1)}, f32[4,16,256]{2,1,0:T(8,128)S(1)}...) custom-call(f32[32,128,256]{2,1,0:T(8,128)} %density.1, ...), custom_call_target="tpu_custom_call" | custom-call | tf_op jit(solution)/shard_map/pallas_call | solution.py:588
  53.3 3.9 %shard_map.42 = (f32[8,128,1024]{2,1,0:T(8,128)}, f32[8,128,1024]{2,1,0:T(8,128)}) custom-call(f32[7,128,1024]{2,1,0:T(8,128)S(1)} %get-tuple-element.9.fstage, f32[7,128,1024]{2,1,0:T(8,128)S(1)} %get-tuple-element.10.pstage, f32[4,128,256]{2,1,0:T(8,128)S(1)} %get-tuple-element.11.lrecv, f32[4,16,256]{2,1,0:T(8,128)S(1)} %get-tuple-element.12.lyb, ...), custom_call_target="tpu_custom_call" | custom-call | tf_op jit(solution)/shard_map/pallas_call | solution.py:618
